TPU v7x, 32 devices: a whole 2x2x4 slice. The times are simulated.
32 devices in a mesh: expert: 16 (over z, y, x), dp: 2 (over core).
Axes of the slice: x: 2, y: 2, z: 4, core: 2. Of those that a mesh axis runs over, the one named last changes fastest.
Arguments:
- tokens: bfloat16 [4096, 1440], P(('expert', 'dp')), may hold values from -6 to 6
- cotangent: bfloat16 [4096, 1440], P(('expert', 'dp')), may hold values from -0.3984375 to 0.3984375
- expert_ids: int32 [4096, 4], P(('expert', 'dp')), may hold values from 0 to 15, all different within a row; in each aligned block of 128 rows (0 to 127, 128 to 255, ...) at most 48 rows name the same one
- gate_weights: float32 [4096, 4], P(('expert', 'dp')), may hold values from 0.05 to 1
- w_gate: bfloat16 [16, 1440, 1440], P('expert', 'dp'), may hold values from -0.15625 to 0.15625
- w_up: bfloat16 [16, 1440, 1440], P('expert', 'dp'), may hold values from -0.15625 to 0.15625
- w_down: bfloat16 [16, 1440, 1440], P('expert', 'dp'), may hold values from -0.15625 to 0.15625
Outputs:
- mixed: bfloat16 [4096, 1440], P(('expert', 'dp'))
- grad_gate: bfloat16 [16, 1440, 1440], P('expert', 'dp')
- grad_up: bfloat16 [16, 1440, 1440], P('expert', 'dp')
- grad_down: bfloat16 [16, 1440, 1440], P('expert', 'dp')
Inputs may be any that keep to these rules, and one draw needn't show every extreme that they name: `expert_ids`: each row names 4 different experts. Within the rows of one device no expert is named more than 48 times, a bound that some block reaches.
All inputs are finite; a program needn't handle non-finite values.
Results may differ from a plain program's by a relative error of at most 0.013.
Values may be sent and summed in bfloat16 or wider, within the bound.
A program may use at most 128 MiB of HBM per device.

v0:
```python
import functools

import jax
import jax.numpy as jnp
from jax import lax
from jax.experimental import pallas as pl
from jax.experimental.pallas import tpu as pltpu
from jax.sharding import PartitionSpec as P


CAP = 512
INNER = 4
TILE = 512
SWISH_SLOPE = 1.702
F32 = jnp.float32
BF16 = jnp.bfloat16


def dot(a, b):
    return jnp.dot(a, b, preferred_element_type=F32)


def dot_nt(a, b):
    return lax.dot_general(a, b, (((1,), (1,)), ((), ())), preferred_element_type=F32)


def dot_tn(a, b):
    return lax.dot_general(a, b, (((0,), (0,)), ((), ())), preferred_element_type=F32)


def share_kernel(size, x_ref, all_ref, send_sem, recv_sem):
    me = lax.axis_index("expert")
    barrier = pltpu.get_barrier_semaphore()
    for k in range(1, size):
        pl.semaphore_signal(
            barrier, inc=1, device_id={"expert": lax.rem(me + k, size)},
            device_id_type=pl.DeviceIdType.MESH,
        )
    pl.semaphore_wait(barrier, size - 1)
    copies = []
    for k in range(1, size):
        copy = pltpu.make_async_remote_copy(
            src_ref=x_ref, dst_ref=all_ref.at[me],
            send_sem=send_sem.at[k], recv_sem=recv_sem.at[k],
            device_id={"expert": lax.rem(me + k, size)},
            device_id_type=pl.DeviceIdType.MESH,
        )
        copy.start()
        copies.append(copy)
    all_ref[me] = x_ref[...]
    for copy in copies:
        copy.wait()


def share(x):
    size = lax.axis_size("expert")
    return pl.pallas_call(
        functools.partial(share_kernel, size),
        out_shape=jax.ShapeDtypeStruct((size,) + x.shape, x.dtype),
        in_specs=[pl.BlockSpec(memory_space=pltpu.VMEM)],
        out_specs=pl.BlockSpec(memory_space=pltpu.VMEM),
        scratch_shapes=[
            pltpu.SemaphoreType.DMA((size,)),
            pltpu.SemaphoreType.DMA((size,)),
        ],
        compiler_params=pltpu.CompilerParams(collective_id=0, has_side_effects=True),
    )(x)


def layer(tokens, cotangent, expert_ids, gate_weights, w_gate, w_up, w_down):
    size = lax.axis_size("expert")
    rows, top = expert_ids.shape
    width = tokens.shape[1]
    slot = 3 * rows * top // (2 * size)
    inner = min(INNER, size)
    outer = size // inner
    me = lax.axis_index("expert")
    mine_out, mine_in = me // inner, me % inner
    half = outer // 2
    partner = jnp.bitwise_xor(mine_in, jnp.arange(inner, dtype=jnp.int32))

    def shift(x, by):
        pairs = [(d, (d // inner + by) % outer * inner + d % inner) for d in range(size)]
        return lax.ppermute(x, "expert", pairs)

    def gather_outer(x):
        blocks = [x] + [None] * (outer - 1)
        for r in range(1, half + 1):
            if outer > 1:
                blocks[r] = shift(blocks[r - 1], 1)
        for r in range(1, outer - half):
            blocks[outer - r] = shift(blocks[(outer - r + 1) % outer], -1)
        return blocks

    def exchange(blocks):
        moved = list(blocks)
        for d in range(inner - 1, 0, -1):
            pairs = [(e, e // inner * inner + (e % inner ^ d)) for e in range(size)]
            moved[d] = lax.ppermute(blocks[d], "expert", pairs)
        return jnp.concatenate(moved)

    def relay(blocks):
        held = jnp.concatenate(blocks)
        return exchange([dot(part, held).astype(BF16) for part in select])

    meta = jnp.concatenate([expert_ids.T.astype(F32), gate_weights.T], axis=0)
    meta_all = share(meta)
    meta_all, tokens = lax.optimization_barrier((meta_all, tokens))
    token_blocks = gather_outer(tokens)
    token_blocks, cotangent = lax.optimization_barrier((token_blocks, cotangent))
    cot_blocks = gather_outer(cotangent)

    ids_all = meta_all[:, :top, :].astype(jnp.int32)
    gates_all = meta_all[:, top:, :]
    back = (mine_out - jnp.arange(outer, dtype=jnp.int32)) % outer

    before = (jnp.arange(rows)[:, None] < jnp.arange(rows)[None, :]).astype(BF16)

    ids_relay = jnp.stack([
        lax.dynamic_index_in_dim(ids_all, back[r] * inner + mine_in, 0, keepdims=False)
        for r in range(outer)
    ])
    near = mine_out * inner + partner
    named = jnp.any(ids_relay[None] == near[:, None, None, None], axis=2)
    rank = dot(named.astype(BF16).reshape(inner * outer, rows), before)
    rank = rank.reshape(inner, outer, rows).astype(jnp.int32)
    place = jnp.where(named, rank, slot)
    hit = place[:, :, None, :] == jnp.arange(slot, dtype=jnp.int32)[None, None, :, None]
    same = jnp.eye(outer, dtype=jnp.bool_)
    select = (hit[:, :, :, None, :] & same[None, :, None, :, None]).astype(BF16)
    select = select.reshape(inner, outer * slot, outer * rows)

    mask = jnp.any(ids_all == me, axis=1)
    gate_of = jnp.sum(jnp.where(ids_all == me, gates_all, 0.0), axis=1)
    counts = jnp.sum(mask.astype(jnp.int32), axis=1)
    below = jnp.arange(size)[:, None] > jnp.arange(size)[None, :]
    starts = jnp.sum(jnp.where(below, counts[None, :], 0), axis=1)
    own_rank = dot(mask.astype(BF16), before).astype(jnp.int32)
    position = jnp.where(mask, starts[:, None] + own_rank, CAP).reshape(1, size * rows)
    row_index = jnp.arange(CAP, dtype=jnp.int32)
    row_gate = jnp.sum(
        jnp.where(position == row_index[:, None], gate_of.reshape(1, size * rows), 0.0),
        axis=1, keepdims=True,
    )
    source = back[None, :] * inner + partner[:, None]
    is_source = source[:, :, None] == jnp.arange(size, dtype=jnp.int32)
    slot_start = jnp.sum(jnp.where(is_source, starts, 0), axis=2)
    slot_live = jnp.sum(jnp.where(is_source, counts, 0), axis=2)
    within = jnp.arange(slot, dtype=jnp.int32)
    slot_row = jnp.where(
        within < slot_live[:, :, None], slot_start[:, :, None] + within, CAP
    ).reshape(1, inner * outer * slot)
    pack = (row_index[:, None] == slot_row).astype(BF16)

    full_gate, full_up, full_down = (
        lax.all_gather(w_gate, "dp", axis=1, tiled=True)[0],
        lax.all_gather(w_up, "dp", axis=1, tiled=True)[0],
        lax.all_gather(w_down, "dp", axis=1, tiled=True)[0],
    )

    recv_x = relay(token_blocks)
    packed_x = dot(pack, recv_x).astype(BF16)
    pre_gate = dot(packed_x, full_gate)
    pre_up = dot(packed_x, full_up)
    sig = jax.nn.sigmoid(SWISH_SLOPE * pre_gate)
    value = pre_gate * sig
    slope = sig + SWISH_SLOPE * pre_gate * sig * (1.0 - sig)
    hidden = (value * (pre_up + 1.0)).astype(BF16)
    out = (dot_nt(hidden, full_down) * row_gate).astype(BF16)
    spread = dot_tn(pack, out).astype(BF16).reshape(inner, outer * slot, width)

    recv_g = relay(cot_blocks)
    spread, recv_g = lax.optimization_barrier((spread, recv_g))
    returned = exchange([spread[d] for d in range(inner)])
    packed_g = (dot(pack, recv_g) * row_gate).astype(BF16)
    grad_down = dot_tn(packed_g, hidden).astype(BF16)
    d_hidden = dot(packed_g, full_down)
    d_gate = (d_hidden * (pre_up + 1.0) * slope).astype(BF16)
    d_up = (d_hidden * value).astype(BF16)
    returned, d_gate, d_up = lax.optimization_barrier((returned, d_gate, d_up))
    partial = dot_tn(select.reshape(inner * outer * slot, outer * rows), returned)
    partial = partial.reshape(outer, rows, width)
    partial, d_gate, d_up = lax.optimization_barrier((partial, d_gate, d_up))
    grad_gate = dot_tn(packed_x, d_gate).astype(BF16)
    grad_up = dot_tn(packed_x, d_up).astype(BF16)

    total = partial[0]
    ahead = partial[half]
    behind = partial[half + 1] if outer - half > 1 else None
    for r in range(half - 1, -1, -1):
        ahead = shift(ahead.astype(BF16), -1).astype(F32)
        if r > 0:
            ahead = ahead + partial[r]
    for r in range(half + 2, outer + 1):
        behind = shift(behind.astype(BF16), 1).astype(F32)
        if r < outer:
            behind = behind + partial[r]
    if half > 0:
        total = total + ahead
    if behind is not None:
        total = total + behind
    mixed = total.astype(BF16)

    grads = [
        lax.psum_scatter(g, "dp", scatter_dimension=0, tiled=True)[None]
        for g in (grad_down, grad_gate, grad_up)
    ]
    return mixed, grads[1], grads[2], grads[0]


def flip(i, d):
    out, bit = 0, 1
    while bit <= max(d, INNER - 1):
        out = out + lax.rem(lax.rem(i // bit, 2) + (d // bit) % 2, 2) * bit
        bit *= 2
    return out


def step_kernel(
    dims, tok_in, cot_in, meta_in, order_in, wg_in, wu_in, wd_in,
    mixed_out, gd_out, gg_out, gu_out,
    col, meta, sel, send, recv, back, pack, x, act, out, g, coef, w, xt, dact,
    zin, zout, near, mask, gq, start, count, place, row_gate,
    load_sem, z_send, z_recv, m_send, m_recv, ms_send, ms_recv, p_send, p_recv,
    w_send, w_recv, r_send, r_recv, g_send, g_recv, o_sem, free_sem,
):
    size, outer, inner, rows, width, top, slot, shard = dims
    span = inner * slot
    me = lax.axis_index("expert")
    dp = lax.axis_index("dp")
    mo, mi = me // inner, lax.rem(me, inner)
    pal = [flip(mi, d) + mo * inner for d in range(inner)]
    other = 1 - dp
    has_up, has_dn = mo < outer - 1, mo > 0
    mesh_id = pl.DeviceIdType.MESH

    def remote(src, dst, ss, rs, device):
        return pltpu.make_async_remote_copy(
            src_ref=src, dst_ref=dst, send_sem=ss, recv_sem=rs,
            device_id=device, device_id_type=mesh_id,
        )

    def tiles(fn):
        full = width // TILE
        if full:
            def step(i, carry):
                fn(pl.ds(pl.multiple_of(i * TILE, TILE), TILE))
                return carry

            lax.fori_loop(0, full, step, 0)
        if width % TILE:
            fn(pl.ds(full * TILE, width % TILE))

    own_rows = pl.ds(pl.multiple_of(dp * shard, 16), shard)
    loads = [
        pltpu.make_async_copy(tok_in, col.at[0, mo], load_sem.at[0]),
        pltpu.make_async_copy(cot_in, col.at[1, mo], load_sem.at[1]),
        pltpu.make_async_copy(meta_in, meta.at[mo, 0], load_sem.at[2]),
    ]
    w_ins = (wd_in, wg_in, wu_in)
    w_loads = [
        pltpu.make_async_copy(w_ins[k].at[0], w.at[k, own_rows], load_sem.at[3 + k])
        for k in range(3)
    ]
    for c in loads + w_loads:
        c.start()

    barrier = pltpu.get_barrier_semaphore()
    for d in range(1, inner):
        pl.semaphore_signal(barrier, inc=1, device_id={"expert": pal[d]}, device_id_type=mesh_id)
    pl.semaphore_signal(barrier, inc=1, device_id={"dp": other}, device_id_type=mesh_id)

    @pl.when(has_up)
    def _():
        pl.semaphore_signal(barrier, inc=1, device_id={"expert": me + inner}, device_id_type=mesh_id)

    @pl.when(has_dn)
    def _():
        pl.semaphore_signal(barrier, inc=1, device_id={"expert": me - inner}, device_id_type=mesh_id)

    pl.semaphore_wait(
        barrier, inner + has_up.astype(jnp.int32) + has_dn.astype(jnp.int32)
    )

    for c in loads:
        c.wait()

    def z_copy(kind, way, r):
        b = mo - r if way == 0 else mo + r
        to = me + inner if way == 0 else me - inner
        if kind == 2:
            return remote(meta.at[b, 0], meta.at[b, 0], ms_send.at[way, r], ms_recv.at[way, r], {"expert": to})
        return remote(
            col.at[kind, b], col.at[kind, b], z_send.at[kind, way, r], z_recv.at[kind, way, r], {"expert": to}
        )

    def sends_z(way, r):
        if way == 0:
            return jnp.logical_and(mo >= r, has_up)
        return jnp.logical_and(mo + r < outer, has_dn)

    def gets_z(way, r):
        return mo >= r + 1 if way == 0 else mo + r + 1 < outer

    def z_wait(kind, way, r):
        b = mo - 1 - r if way == 0 else mo + 1 + r
        frm = me - inner if way == 0 else me + inner
        if kind == 2:
            remote(meta.at[b, 0], meta.at[b, 0], ms_send.at[way, r], ms_recv.at[way, r], {"expert": frm}).wait_recv()
        else:
            remote(
                col.at[kind, b], col.at[kind, b], z_send.at[kind, way, r], z_recv.at[kind, way, r], {"expert": frm}
            ).wait_recv()

    def z_issue_tok(way, r):
        @pl.when(sends_z(way, r))
        def _():
            z_copy(2, way, r).start()
            z_copy(0, way, r).start()
            last = mo == r if way == 0 else mo + r == outer - 1

            @pl.when(last)
            def _():
                z_copy(1, way, 0).start()

    for way in (0, 1):
        z_issue_tok(way, 0)

    def w_copy(k):
        return remote(w_ins[k].at[0], w.at[k, own_rows], w_send.at[k], w_recv.at[k], {"dp": other})

    for k in (1, 2, 0):
        w_copy(k).start()

    sub = lax.broadcasted_iota(jnp.int32, (8, rows), 0)
    wanted = jnp.full((8, rows), -7, jnp.int32)
    for d in range(inner):
        wanted = jnp.where(sub == d, pal[d], wanted)
    near[...] = wanted.astype(F32)

    def earlier():
        a = lax.broadcasted_iota(jnp.int32, (rows, rows), 0)
        b = lax.broadcasted_iota(jnp.int32, (rows, rows), 1)
        return jnp.where(a < b, 1.0, 0.0).astype(BF16)

    def build(b):
        ids = meta[b, 0, 0:8, :]
        named = jnp.zeros((8, rows), F32)
        for k in range(top):
            named = named + jnp.where(ids[k:k + 1, :] == near[...], 1.0, 0.0)
        rank = dot(named.astype(BF16), earlier())
        spot = jnp.where(named > 0.0, rank, float(slot))
        within = lax.broadcasted_iota(jnp.int32, (slot, rows), 0).astype(F32)
        for d in range(inner):
            sel[b, d * slot:(d + 1) * slot, :] = jnp.where(spot[d:d + 1, :] == within, 1.0, 0.0).astype(BF16)

    def m_copy(b, d):
        return remote(meta.at[b, 0], meta.at[b, d], m_send.at[b, d], m_recv.at[b, d], {"expert": pal[d]})

    def p_copy(kind, b, d):
        part = pl.ds(d * slot, slot)
        dst = recv.at[kind, b, part] if kind < 2 else back.at[b, part]
        src = send.at[kind, b, part] if kind < 2 else send.at[0, b, part]
        return remote(src, dst, p_send.at[kind, b, d], p_recv.at[kind, b, d], {"expert": pal[d]})

    def scatter(kind, b):
        picked = dot(sel[b], col[kind, b]).astype(BF16)
        send[kind, b, slot:, :] = picked[slot:, :]
        recv[kind, b, :slot, :] = picked[:slot, :]
        for d in range(1, inner):
            p_copy(kind, b, d).start()

    def spread_tok(b):
        for d in range(1, inner):
            m_copy(b, d).start()
        build(b)
        scatter(0, b)

    spread_tok(mo)
    scatter(1, mo)
    for r in range(outer - 1):
        for way in (0, 1):
            @pl.when(gets_z(way, r))
            def _():
                z_wait(2, way, r)
                z_wait(0, way, r)
                if r + 1 < outer - 1:
                    z_issue_tok(way, r + 1)
        for way in (0, 1):
            @pl.when(gets_z(way, r))
            def _():
                spread_tok(mo - 1 - r if way == 0 else mo + 1 + r)

    def cot_round(r):
        for way in (0, 1):
            @pl.when(gets_z(way, r))
            def _():
                z_wait(1, way, r)
                if r + 1 < outer - 1:
                    @pl.when(sends_z(way, r + 1))
                    def _():
                        z_copy(1, way, r + 1).start()
        for way in (0, 1):
            @pl.when(gets_z(way, r))
            def _():
                scatter(1, mo - 1 - r if way == 0 else mo + 1 + r)

    for b in range(outer):
        for d in range(1, inner):
            m_copy(b, d).wait_recv()
    mine = jnp.full((8, rows), me, jnp.int32).astype(F32)
    for b in range(outer):
        for d in range(inner):
            q = b * inner + d
            same = meta[b, d, 0:8, :] == mine
            mask[q:q + 1, :] = jnp.sum(jnp.where(same, 1.0, 0.0), axis=0, keepdims=True)
            gq[q:q + 1, :] = jnp.sum(jnp.where(same, meta[b, d, 8:16, :], 0.0), axis=0, keepdims=True)
    held = mask[...].astype(BF16)
    ones = jnp.ones((rows, rows), BF16)
    begin = dot(dot(order_in[...], held).astype(BF16), ones)
    start[...] = begin
    count[...] = dot(held, ones)
    place[...] = jnp.where(mask[...] > 0.0, begin + dot(held, earlier()), float(CAP))
    within = lax.broadcasted_iota(jnp.int32, (slot, 128), 0).astype(F32)
    lane = lax.broadcasted_iota(jnp.int32, (slot, 128), 1).astype(F32)
    for q in range(size):
        target = jnp.where(within < count[q:q + 1, :128], start[q:q + 1, :128] + within, float(CAP))
        for j in range(CAP // 128):
            pack[q * slot:(q + 1) * slot, j * 128:(j + 1) * 128] = jnp.where(
                target == lane + float(j * 128), 1.0, 0.0
            ).astype(BF16)
    down = lax.broadcasted_iota(jnp.int32, (128, rows), 0).astype(F32)
    for j in range(CAP // 128):
        acc = jnp.zeros((128, rows), F32)
        for q in range(size):
            acc = acc + jnp.where(place[q:q + 1, :] == down + float(j * 128), gq[q:q + 1, :], 0.0)
        row_gate[j * 128:(j + 1) * 128, :] = jnp.broadcast_to(jnp.sum(acc, axis=1, keepdims=True), (128, 128))

    for b in range(outer):
        for d in range(1, inner):
            p_copy(0, b, d).wait_recv()

    def gather(kind, n):
        return dot_tn(pack[...], recv[kind, :, :, n].reshape(outer * span, n.size))

    def pack_x(n):
        x[:, n] = gather(0, n).astype(BF16)

    tiles(pack_x)
    cot_round(0)

    for k in (1, 2):
        w_loads[k].wait()
        w_copy(k).wait_recv()

    def forward(n):
        pre_gate = dot(x[...], w[1, :, n])
        pre_up = dot(x[...], w[2, :, n]) + 1.0
        sig = jax.nn.sigmoid(SWISH_SLOPE * pre_gate)
        value = pre_gate * sig
        slope = sig + SWISH_SLOPE * value * (1.0 - sig)
        act[:, n] = (value * pre_up).astype(BF16)
        coef[0, :, n] = pre_up * slope
        coef[1, :, n] = value

    tiles(forward)
    if outer > 2:
        cot_round(1)

    w_loads[0].wait()
    w_copy(0).wait_recv()

    def project(n):
        out[:, n] = (dot_nt(act[...], w[0, n, :]) * row_gate[:, :1]).astype(BF16)

    tiles(project)
    for r in range(2, outer - 1):
        cot_round(r)

    for b in range(outer):
        for d in range(1, inner):
            p_copy(0, b, d).wait_send()

    def give_back(b):
        part = pl.ds(pl.multiple_of(b * span, 16), span)
        rows_back = dot(pack[part, :], out[...]).astype(BF16)
        send[0, b, slot:, :] = rows_back[slot:, :]
        back[b, :slot, :] = rows_back[:slot, :]
        for d in range(1, inner):
            p_copy(2, b, d).start()

    for r in range(outer - 1, -1, -1):
        @pl.when(mo >= r)
        def _():
            give_back(mo - r)

        if r > 0:
            @pl.when(mo + r < outer)
            def _():
                give_back(mo + r)

    def flip_x(n):
        xt[1, n, :] = dot_tn(x[:, n], unit()).astype(BF16)

    def unit():
        a = lax.broadcasted_iota(jnp.int32, (CAP, CAP), 0)
        b = lax.broadcasted_iota(jnp.int32, (CAP, CAP), 1)
        return jnp.where(a == b, 1.0, 0.0).astype(BF16)

    tiles(flip_x)

    for b in range(outer):
        for d in range(1, inner):
            p_copy(1, b, d).wait_recv()

    def pack_g(n):
        g[:, n] = (gather(1, n) * row_gate[:, :1]).astype(BF16)

    tiles(pack_g)

    def flip_g(n):
        xt[0, n, :] = dot_tn(g[:, n], unit()).astype(BF16)

    tiles(flip_g)

    def back_act(n):
        d_hidden = dot(g[...], w[0, :, n])
        dact[0, :, n] = (d_hidden * coef[0, :, n]).astype(BF16)
        dact[1, :, n] = (d_hidden * coef[1, :, n]).astype(BF16)

    tiles(back_act)
    pl.semaphore_signal(free_sem, inc=1, device_id={"dp": other}, device_id_type=mesh_id)

    def r_copy(way, r):
        to = me - inner if way == 0 else me + inner
        return remote(
            zout.at[way, r - 1], zin.at[way, r - 1], r_send.at[way, r - 1], r_recv.at[way, r - 1], {"expert": to}
        )

    def partial(b):
        for d in range(1, inner):
            p_copy(2, b, d).wait_recv()
        return dot_tn(sel[b], back[b])

    def ret_round(r):
        for way in (0, 1):
            b = mo - r if way == 0 else mo + r
            inbound = has_up if way == 0 else has_dn
            if way == 1:
                inbound = mo > 0

            @pl.when(mo >= r if way == 0 else mo + r < outer)
            def _():
                zout[way, r - 1] = partial(b).astype(BF16)
                if r < outer - 1:
                    @pl.when(inbound)
                    def _():
                        r_copy(way, r + 1).wait_recv()
                        zout[way, r - 1] = (
                            zout[way, r - 1].astype(F32) + zin[way, r].astype(F32)
                        ).astype(BF16)
                r_copy(way, r).start()

    def ret_last():
        mixed_out[...] = partial(mo).astype(BF16)
        for way in (0, 1):
            @pl.when(has_up if way == 0 else has_dn)
            def _():
                r_copy(way, 1).wait_recv()
                mixed_out[...] = (mixed_out[...].astype(F32) + zin[way, 0].astype(F32)).astype(BF16)

    send_rows = pl.ds(0, shard)
    recv_rows = pl.ds(shard, shard)

    def g_copy(k):
        return remote(
            w.at[k, send_rows], w.at[k, recv_rows], g_send.at[k], g_recv.at[k], {"dp": other}
        )

    def right(k, n):
        return act[:, n] if k == 0 else dact[k - 1, :, n]

    their_rows = pl.ds(pl.multiple_of(other * shard, 16), shard)
    for r in range(outer - 1, 1, -1):
        ret_round(r)
    for k in range(3):
        lhs = 0 if k == 0 else 1

        def theirs(n):
            w[k, send_rows, n] = dot(xt[lhs, their_rows, :], right(k, n)).astype(BF16)

        tiles(theirs)
        if k == 0:
            pl.semaphore_wait(free_sem, 1)
        g_copy(k).start()
        if k == 0 and outer > 1:
            ret_round(1)
    ret_last()
    outs = (gd_out, gg_out, gu_out)
    stores = []
    for k in range(3):
        lhs = 0 if k == 0 else 1
        g_copy(k).wait_recv()

        def ours(n):
            total = dot(xt[lhs, own_rows, :], right(k, n)) + w[k, recv_rows, n].astype(F32)
            w[k, recv_rows, n] = total.astype(BF16)

        tiles(ours)
        store = pltpu.make_async_copy(w.at[k, recv_rows], outs[k].at[0], o_sem.at[k])
        store.start()
        stores.append(store)

    for way in (0, 1):
        for r in range(outer - 1):
            @pl.when(sends_z(way, r))
            def _():
                for kind in (0, 1, 2):
                    z_copy(kind, way, r).wait_send()
        for r in range(1, outer):
            @pl.when(mo >= r if way == 0 else mo + r < outer)
            def _():
                r_copy(way, r).wait_send()
    for b in range(outer):
        for d in range(1, inner):
            m_copy(b, d).wait_send()
            p_copy(1, b, d).wait_send()
            p_copy(2, b, d).wait_send()
    for k in range(3):
        w_copy(k).wait_send()
        g_copy(k).wait_send()
        stores[k].wait()


def fits(args):
    rows = args[0].shape[0]
    shard = args[4].shape[1]
    size = lax.axis_size("expert")
    return (
        lax.axis_size("dp") == 2 and shard % 16 == 0 and rows == 128
        and size % INNER == 0 and INNER < size <= 16
    )


def fused_layer(tokens, cotangent, expert_ids, gate_weights, w_gate, w_up, w_down):
    size = lax.axis_size("expert")
    rows, top = expert_ids.shape
    width = tokens.shape[1]
    shard = w_gate.shape[1]
    hid = w_gate.shape[2]
    inner = INNER
    outer = size // inner
    slot = -(-3 * rows * top // (2 * size) // 16) * 16
    span = inner * slot
    me = lax.axis_index("expert")
    meta = jnp.concatenate([
        jnp.pad(expert_ids.T.astype(F32), ((0, 8 - top), (0, 0)), constant_values=-1.0),
        jnp.pad(gate_weights.T, ((0, 8 - top), (0, 0))),
    ], axis=0)
    which = jnp.arange(size, dtype=jnp.int32)
    source = which // inner * inner + jnp.bitwise_xor(me % inner, which % inner)
    order = (source[None, :] < source[:, None]).astype(BF16)
    dims = (size, outer, inner, rows, width, top, slot, shard)
    anywhere = pl.BlockSpec(memory_space=pl.ANY)
    vmem = pl.BlockSpec(memory_space=pltpu.VMEM)
    dma = pltpu.SemaphoreType.DMA
    hop = outer - 1
    scratch = [
        pltpu.VMEM((2, outer, rows, width), BF16),
        pltpu.VMEM((outer, inner, 16, rows), F32),
        pltpu.VMEM((outer, span, rows), BF16),
        pltpu.VMEM((2, outer, span, width), BF16),
        pltpu.VMEM((2, outer, span, width), BF16),
        pltpu.VMEM((outer, span, width), BF16),
        pltpu.VMEM((outer * span, CAP), BF16),
        pltpu.VMEM((CAP, width), BF16),
        pltpu.VMEM((CAP, hid), BF16),
        pltpu.VMEM((CAP, width), BF16),
        pltpu.VMEM((CAP, width), BF16),
        pltpu.VMEM((2, CAP, hid), F32),
        pltpu.VMEM((3, 2 * shard, hid), BF16),
        pltpu.VMEM((2, width, CAP), BF16),
        pltpu.VMEM((2, CAP, hid), BF16),
        pltpu.VMEM((2, hop, rows, width), BF16),
        pltpu.VMEM((2, hop, rows, width), BF16),
        pltpu.VMEM((8, rows), F32),
        pltpu.VMEM((size, rows), F32),
        pltpu.VMEM((size, rows), F32),
        pltpu.VMEM((size, rows), F32),
        pltpu.VMEM((size, rows), F32),
        pltpu.VMEM((size, rows), F32),
        pltpu.VMEM((CAP, 128), F32),
        dma((6,)), dma((2, 2, hop)), dma((2, 2, hop)),
        dma((outer, inner)), dma((outer, inner)), dma((2, hop)), dma((2, hop)),
        dma((3, outer, inner)), dma((3, outer, inner)),
        dma((3,)), dma((3,)), dma((2, hop)), dma((2, hop)), dma((3,)), dma((3,)), dma((3,)),
        pltpu.SemaphoreType.REGULAR,
    ]
    grad = jax.ShapeDtypeStruct(w_gate.shape, BF16)
    mixed, gd, gg, gu = pl.pallas_call(
        functools.partial(step_kernel, dims),
        out_shape=(jax.ShapeDtypeStruct((rows, width), BF16), grad, grad, grad),
        in_specs=[anywhere, anywhere, anywhere, vmem, anywhere, anywhere, anywhere],
        out_specs=(vmem, anywhere, anywhere, anywhere),
        scratch_shapes=scratch,
        compiler_params=pltpu.CompilerParams(
            collective_id=1, has_side_effects=True, vmem_limit_bytes=67043328
        ),
    )(tokens, cotangent, meta, order, w_gate, w_up, w_down)
    return mixed, gg, gu, gd


def body(*args):
    if fits(args):
        return fused_layer(*args)
    return layer(*args)


def solution(mesh):
    rows = P(("expert", "dp"), None)
    mats = P("expert", "dp", None)
    return jax.shard_map(
        body,
        mesh=mesh,
        in_specs=(rows, rows, rows, rows, mats, mats, mats),
        out_specs=(rows, mats, mats, mats),
        check_vma=False,
    )
```

profile of v0, /device:TPU:0, one launch (start us, length us, event | category | flops | bytes accessed | tf_op | source)
XLA Modules:
  0.0 130.7 jit_solution(5539338648500087244)
XLA Ops:
  0.7 0.7 convert_bitcast_fusion
  1.3 0.7 compare_convert_fusion.order_in
  2.0 1.3 select_maximum_fusion.meta_in
  3.3 1.9 %copy.11.tok_in = bf16[128,1440]{1,0:T(8,128)(2,1)} copy(bf16[128,1440]{0,1:T(8,128)(2,1)} %param.7) | data formatting | bytes 737280 | tf_op args[0]
  5.2 1.9 %copy.12.cot_in = bf16[128,1440]{1,0:T(8,128)(2,1)} copy(bf16[128,1440]{0,1:T(8,128)(2,1)} %param.8) | data formatting | bytes 737280 | tf_op args[1]
  7.1 114.6 %shard_map.102 = (bf16[128,1440]{1,0:T(8,128)(2,1)}, bf16[1,720,1440]{2,1,0:T(8,128)(2,1)}, bf16[1,720,1440]{2,1,0:T(8,128)(2,1)}, bf16[1,720,1440]{2,1,0:T(8,128)(2,1)}) custom-call(bf16[128,1440]{1,0:T(8,128)(2,1)} %copy.11.tok_in, bf16[128,1440]{1,0:T(8,128)(2,1)} %copy.12.cot_in, f32[16,128]{1,0:T(8,128)} %select_maximum_fusion.meta_in, ...), custom_call_target="tpu_custom_call" | custom-call | tf_op jit(solution)/shard_map/pallas_call | solution.py:700
  121.7 1.9 %copy.13 = bf16[128,1440]{0,1:T(8,128)(2,1)} copy(bf16[128,1440]{1,0:T(8,128)(2,1)} %get-tuple-element.12) | data formatting | bytes 737280
  123.6 0.0 copy-start.1
  123.6 3.3 %copy.17 = bf16[1,720,1440]{2,1,0:T(8,128)(2,1)} copy(bf16[1,720,1440]{2,1,0:T(8,128)(2,1)} %get-tuple-element.21) | data formatting | bytes 4147200
  126.9 0.0 copy-done.1
  126.9 0.0 copy-start
  126.9 1.4 %copy.18 = bf16[1,720,1440]{2,1,0:T(8,128)(2,1)} copy(bf16[1,720,1440]{2,1,0:T(8,128)(2,1)S(1)} %copy-done.1) | data formatting | bytes 4147200
  128.2 1.1 copy-done
  129.3 1.4 %copy.19 = bf16[1,720,1440]{2,1,0:T(8,128)(2,1)} copy(bf16[1,720,1440]{2,1,0:T(8,128)(2,1)S(1)} %copy-done) | data formatting | bytes 4147200
  (1 shorter events, 0.0 us)
Async XLA Ops:
  123.6 3.3 %copy-start.1 = (bf16[1,720,1440]{2,1,0:T(8,128)(2,1)S(1)}, bf16[1,720,1440]{2,1,0:T(8,128)(2,1)}, u32[]{:S(2)}) copy-start(bf16[1,720,1440]{2,1,0:T(8,128)(2,1)} %get-tuple-element.22) | copy-start | bytes 6220804
  126.9 2.4 %copy-start = (bf16[1,720,1440]{2,1,0:T(8,128)(2,1)S(1)}, bf16[1,720,1440]{2,1,0:T(8,128)(2,1)}, u32[]{:S(2)}) copy-start(bf16[1,720,1440]{2,1,0:T(8,128)(2,1)} %get-tuple-element.23) | copy-start | bytes 6220804
where the time goes:
time: 131 us
  Pallas kernels  115 us (88%)
  local copies, waits for them, and re-layouts  12.8 us (10%)
  other arithmetic  2.64 us (2%)
    pallas_call x1, Pallas kernels, fused_layer(): pl.pallas_call(functools.partial(step_kernel, dims), out_shape=(jax.Shape...  115 us
    unnamed x10, local copies, waits for them, and re-layouts  12.8 us

commit v1 on v0

--- a/solution.py
+++ b/solution.py
@@ -11,6 +11,7 @@
 CAP = 512
 INNER = 4
 TILE = 512
+PIECES = 2
 SWISH_SLOPE = 1.702
 F32 = jnp.float32
 BF16 = jnp.bfloat16
@@ -217,12 +218,12 @@
 
 
 def step_kernel(
-    dims, tok_in, cot_in, meta_in, order_in, wg_in, wu_in, wd_in,
+    dims, tok_in, cot_in, ids_in, gates_in, wg_in, wu_in, wd_in,
     mixed_out, gd_out, gg_out, gu_out,
-    col, meta, sel, send, recv, back, pack, x, act, out, g, coef, w, xt, dact,
-    zin, zout, near, mask, gq, start, count, place, row_gate,
+    ids_buf, gates_buf, col, meta, sel, send, recv, back, pack, x, act, out, g, coef, w, xt, dact,
+    zin, zout, near, mask, gq, start, count, place, row_gate, total,
     load_sem, z_send, z_recv, m_send, m_recv, ms_send, ms_recv, p_send, p_recv,
-    w_send, w_recv, r_send, r_recv, g_send, g_recv, o_sem, free_sem,
+    w_send, w_recv, r_send, r_recv, g_send, g_recv, free_sem,
 ):
     size, outer, inner, rows, width, top, slot, shard = dims
     span = inner * slot
@@ -251,11 +252,18 @@
         if width % TILE:
             fn(pl.ds(full * TILE, width % TILE))
 
+    def zero_ends():
+        for way, has in ((0, has_up), (1, has_dn)):
+            @pl.when(jnp.logical_not(has))
+            def _():
+                zin[way, 0] = jnp.zeros((width, rows), BF16)
+
     own_rows = pl.ds(pl.multiple_of(dp * shard, 16), shard)
     loads = [
         pltpu.make_async_copy(tok_in, col.at[0, mo], load_sem.at[0]),
         pltpu.make_async_copy(cot_in, col.at[1, mo], load_sem.at[1]),
-        pltpu.make_async_copy(meta_in, meta.at[mo, 0], load_sem.at[2]),
+        pltpu.make_async_copy(ids_in, ids_buf, load_sem.at[2]),
+        pltpu.make_async_copy(gates_in, gates_buf, load_sem.at[6]),
     ]
     w_ins = (wd_in, wg_in, wu_in)
     w_loads = [
@@ -278,21 +286,30 @@
     def _():
         pl.semaphore_signal(barrier, inc=1, device_id={"expert": me - inner}, device_id_type=mesh_id)
 
+    zero_ends()
+    for c in loads[2:]:
+        c.wait()
+    meta[mo, 0, 0:8, :] = jnp.full((8, rows), -1.0, F32)
+    meta[mo, 0, 8:16, :] = jnp.zeros((8, rows), F32)
+    meta[mo, 0, 0:top, :] = ids_buf[...].astype(F32)
+    meta[mo, 0, 8:8 + top, :] = gates_buf[...]
+    for c in loads[:2]:
+        c.wait()
     pl.semaphore_wait(
         barrier, inner + has_up.astype(jnp.int32) + has_dn.astype(jnp.int32)
     )
 
-    for c in loads:
-        c.wait()
-
-    def z_copy(kind, way, r):
+
+    def piece(h):
+        return pl.ds(h * (width // PIECES), width // PIECES)
+
+    def z_copy(kind, way, r, h=0):
         b = mo - r if way == 0 else mo + r
         to = me + inner if way == 0 else me - inner
         if kind == 2:
             return remote(meta.at[b, 0], meta.at[b, 0], ms_send.at[way, r], ms_recv.at[way, r], {"expert": to})
-        return remote(
-            col.at[kind, b], col.at[kind, b], z_send.at[kind, way, r], z_recv.at[kind, way, r], {"expert": to}
-        )
+        part = col.at[kind, b, piece(h)]
+        return remote(part, part, z_send.at[kind, way, r, h], z_recv.at[kind, way, r, h], {"expert": to})
 
     def sends_z(way, r):
         if way == 0:
@@ -302,29 +319,45 @@
     def gets_z(way, r):
         return mo >= r + 1 if way == 0 else mo + r + 1 < outer
 
-    def z_wait(kind, way, r):
+    def z_wait(kind, way, r, h=0):
         b = mo - 1 - r if way == 0 else mo + 1 + r
         frm = me - inner if way == 0 else me + inner
         if kind == 2:
             remote(meta.at[b, 0], meta.at[b, 0], ms_send.at[way, r], ms_recv.at[way, r], {"expert": frm}).wait_recv()
         else:
+            part = col.at[kind, b, piece(h)]
             remote(
-                col.at[kind, b], col.at[kind, b], z_send.at[kind, way, r], z_recv.at[kind, way, r], {"expert": frm}
+                part, part, z_send.at[kind, way, r, h], z_recv.at[kind, way, r, h], {"expert": frm}
             ).wait_recv()
 
-    def z_issue_tok(way, r):
+    def z_issue(kind, way, r, h):
         @pl.when(sends_z(way, r))
         def _():
-            z_copy(2, way, r).start()
-            z_copy(0, way, r).start()
-            last = mo == r if way == 0 else mo + r == outer - 1
-
-            @pl.when(last)
-            def _():
-                z_copy(1, way, 0).start()
-
-    for way in (0, 1):
-        z_issue_tok(way, 0)
+            if kind == 0 and h == 0:
+                z_copy(2, way, r).start()
+            z_copy(kind, way, r, h).start()
+            if kind == 0 and h == PIECES - 1:
+                last = mo == r if way == 0 else mo + r == outer - 1
+
+                @pl.when(last)
+                def _():
+                    for i in range(PIECES):
+                        z_copy(1, way, 0, i).start()
+
+    def z_round(kind, r):
+        for h in range(PIECES):
+            for way in (0, 1):
+                @pl.when(gets_z(way, r))
+                def _():
+                    if kind == 0 and h == 0:
+                        z_wait(2, way, r)
+                    z_wait(kind, way, r, h)
+                    if r + 1 < outer - 1:
+                        z_issue(kind, way, r + 1, h)
+
+    for h in range(PIECES):
+        for way in (0, 1):
+            z_issue(0, way, 0, h)
 
     def w_copy(k):
         return remote(w_ins[k].at[0], w.at[k, own_rows], w_send.at[k], w_recv.at[k], {"dp": other})
@@ -364,7 +397,7 @@
         return remote(src, dst, p_send.at[kind, b, d], p_recv.at[kind, b, d], {"expert": pal[d]})
 
     def scatter(kind, b):
-        picked = dot(sel[b], col[kind, b]).astype(BF16)
+        picked = dot_nt(sel[b], col[kind, b]).astype(BF16)
         send[kind, b, slot:, :] = picked[slot:, :]
         recv[kind, b, :slot, :] = picked[:slot, :]
         for d in range(1, inner):
@@ -379,31 +412,27 @@
     spread_tok(mo)
     scatter(1, mo)
     for r in range(outer - 1):
-        for way in (0, 1):
-            @pl.when(gets_z(way, r))
-            def _():
-                z_wait(2, way, r)
-                z_wait(0, way, r)
-                if r + 1 < outer - 1:
-                    z_issue_tok(way, r + 1)
+        z_round(0, r)
         for way in (0, 1):
             @pl.when(gets_z(way, r))
             def _():
                 spread_tok(mo - 1 - r if way == 0 else mo + 1 + r)
 
+    at_end = jnp.logical_or(mo == 0, mo == outer - 1)
+    inside = jnp.logical_not(at_end)
+
     def cot_round(r):
-        for way in (0, 1):
-            @pl.when(gets_z(way, r))
-            def _():
-                z_wait(1, way, r)
-                if r + 1 < outer - 1:
-                    @pl.when(sends_z(way, r + 1))
-                    def _():
-                        z_copy(1, way, r + 1).start()
+        z_round(1, r)
         for way in (0, 1):
             @pl.when(gets_z(way, r))
             def _():
                 scatter(1, mo - 1 - r if way == 0 else mo + 1 + r)
+
+    def cot_at(r, when):
+        if r < outer - 1:
+            @pl.when(when)
+            def _():
+                cot_round(r)
 
     for b in range(outer):
         for d in range(1, inner):
@@ -416,8 +445,11 @@
             mask[q:q + 1, :] = jnp.sum(jnp.where(same, 1.0, 0.0), axis=0, keepdims=True)
             gq[q:q + 1, :] = jnp.sum(jnp.where(same, meta[b, d, 8:16, :], 0.0), axis=0, keepdims=True)
     held = mask[...].astype(BF16)
+    first = jnp.bitwise_xor(lax.broadcasted_iota(jnp.int32, (size, size), 0), mi)
+    second = jnp.bitwise_xor(lax.broadcasted_iota(jnp.int32, (size, size), 1), mi)
+    order = jnp.where(second < first, 1.0, 0.0).astype(BF16)
     ones = jnp.ones((rows, rows), BF16)
-    begin = dot(dot(order_in[...], held).astype(BF16), ones)
+    begin = dot(dot(order, held).astype(BF16), ones)
     start[...] = begin
     count[...] = dot(held, ones)
     place[...] = jnp.where(mask[...] > 0.0, begin + dot(held, earlier()), float(CAP))
@@ -436,6 +468,7 @@
             acc = acc + jnp.where(place[q:q + 1, :] == down + float(j * 128), gq[q:q + 1, :], 0.0)
         row_gate[j * 128:(j + 1) * 128, :] = jnp.broadcast_to(jnp.sum(acc, axis=1, keepdims=True), (128, 128))
 
+    cot_at(0, inside)
     for b in range(outer):
         for d in range(1, inner):
             p_copy(0, b, d).wait_recv()
@@ -447,7 +480,8 @@
         x[:, n] = gather(0, n).astype(BF16)
 
     tiles(pack_x)
-    cot_round(0)
+    cot_at(0, at_end)
+    cot_at(1, inside)
 
     for k in (1, 2):
         w_loads[k].wait()
@@ -464,8 +498,7 @@
         coef[1, :, n] = value
 
     tiles(forward)
-    if outer > 2:
-        cot_round(1)
+    cot_at(1, at_end)
 
     w_loads[0].wait()
     w_copy(0).wait_recv()
@@ -474,8 +507,6 @@
         out[:, n] = (dot_nt(act[...], w[0, n, :]) * row_gate[:, :1]).astype(BF16)
 
     tiles(project)
-    for r in range(2, outer - 1):
-        cot_round(r)
 
     for b in range(outer):
         for d in range(1, inner):
@@ -489,7 +520,7 @@
         for d in range(1, inner):
             p_copy(2, b, d).start()
 
-    for r in range(outer - 1, -1, -1):
+    def give_round(r):
         @pl.when(mo >= r)
         def _():
             give_back(mo - r)
@@ -499,6 +530,56 @@
             def _():
                 give_back(mo + r)
 
+    give_round(outer - 1)
+    for r in range(2, outer - 1):
+        cot_round(r)
+    for r in range(outer - 2, -1, -1):
+        give_round(r)
+
+    def r_copy(way, r, h):
+        to = me - inner if way == 0 else me + inner
+        return remote(
+            zout.at[way, r - 1, piece(h)], zin.at[way, r - 1, piece(h)],
+            r_send.at[way, r - 1, h], r_recv.at[way, r - 1, h], {"expert": to},
+        )
+
+    def partial(b):
+        for d in range(1, inner):
+            p_copy(2, b, d).wait_recv()
+        return dot_tn(back[b], sel[b])
+
+    def gives(way, r):
+        return mo >= r if way == 0 else mo + r < outer
+
+    def ret_round(r):
+        for way in (0, 1):
+            @pl.when(gives(way, r))
+            def _():
+                zout[way, r - 1] = partial(mo - r if way == 0 else mo + r).astype(BF16)
+        for h in range(PIECES):
+            for way, inbound in ((0, has_up), (1, has_dn)):
+                @pl.when(gives(way, r))
+                def _():
+                    if r < outer - 1:
+                        @pl.when(inbound)
+                        def _():
+                            r_copy(way, r + 1, h).wait_recv()
+                            zout[way, r - 1, piece(h)] = (
+                                zout[way, r - 1, piece(h)].astype(F32) + zin[way, r, piece(h)].astype(F32)
+                            ).astype(BF16)
+                    r_copy(way, r, h).start()
+
+    def ret_last():
+        total[...] = partial(mo)
+        for h in range(PIECES):
+            for way, inbound in ((0, has_up), (1, has_dn)):
+                @pl.when(inbound)
+                def _():
+                    r_copy(way, 1, h).wait_recv()
+            mixed_out[piece(h)] = (
+                total[piece(h)] + zin[0, 0, piece(h)].astype(F32) + zin[1, 0, piece(h)].astype(F32)
+            ).astype(BF16)
+
     def flip_x(n):
         xt[1, n, :] = dot_tn(x[:, n], unit()).astype(BF16)
 
@@ -508,6 +589,7 @@
         return jnp.where(a == b, 1.0, 0.0).astype(BF16)
 
     tiles(flip_x)
+    ret_round(outer - 1)
 
     for b in range(outer):
         for d in range(1, inner):
@@ -531,44 +613,6 @@
     tiles(back_act)
     pl.semaphore_signal(free_sem, inc=1, device_id={"dp": other}, device_id_type=mesh_id)
 
-    def r_copy(way, r):
-        to = me - inner if way == 0 else me + inner
-        return remote(
-            zout.at[way, r - 1], zin.at[way, r - 1], r_send.at[way, r - 1], r_recv.at[way, r - 1], {"expert": to}
-        )
-
-    def partial(b):
-        for d in range(1, inner):
-            p_copy(2, b, d).wait_recv()
-        return dot_tn(sel[b], back[b])
-
-    def ret_round(r):
-        for way in (0, 1):
-            b = mo - r if way == 0 else mo + r
-            inbound = has_up if way == 0 else has_dn
-            if way == 1:
-                inbound = mo > 0
-
-            @pl.when(mo >= r if way == 0 else mo + r < outer)
-            def _():
-                zout[way, r - 1] = partial(b).astype(BF16)
-                if r < outer - 1:
-                    @pl.when(inbound)
-                    def _():
-                        r_copy(way, r + 1).wait_recv()
-                        zout[way, r - 1] = (
-                            zout[way, r - 1].astype(F32) + zin[way, r].astype(F32)
-                        ).astype(BF16)
-                r_copy(way, r).start()
-
-    def ret_last():
-        mixed_out[...] = partial(mo).astype(BF16)
-        for way in (0, 1):
-            @pl.when(has_up if way == 0 else has_dn)
-            def _():
-                r_copy(way, 1).wait_recv()
-                mixed_out[...] = (mixed_out[...].astype(F32) + zin[way, 0].astype(F32)).astype(BF16)
-
     send_rows = pl.ds(0, shard)
     recv_rows = pl.ds(shard, shard)
 
@@ -581,7 +625,7 @@
         return act[:, n] if k == 0 else dact[k - 1, :, n]
 
     their_rows = pl.ds(pl.multiple_of(other * shard, 16), shard)
-    for r in range(outer - 1, 1, -1):
+    for r in range(outer - 2, 1, -1):
         ret_round(r)
     for k in range(3):
         lhs = 0 if k == 0 else 1
@@ -593,34 +637,34 @@
         if k == 0:
             pl.semaphore_wait(free_sem, 1)
         g_copy(k).start()
-        if k == 0 and outer > 1:
-            ret_round(1)
-    ret_last()
+    if outer > 2:
+        ret_round(1)
     outs = (gd_out, gg_out, gu_out)
-    stores = []
     for k in range(3):
         lhs = 0 if k == 0 else 1
         g_copy(k).wait_recv()
 
         def ours(n):
-            total = dot(xt[lhs, own_rows, :], right(k, n)) + w[k, recv_rows, n].astype(F32)
-            w[k, recv_rows, n] = total.astype(BF16)
+            grad = dot(xt[lhs, own_rows, :], right(k, n)) + w[k, recv_rows, n].astype(F32)
+            outs[k][0, :, n] = grad.astype(BF16)
 
         tiles(ours)
-        store = pltpu.make_async_copy(w.at[k, recv_rows], outs[k].at[0], o_sem.at[k])
-        store.start()
-        stores.append(store)
+
+    ret_last()
 
     for way in (0, 1):
         for r in range(outer - 1):
             @pl.when(sends_z(way, r))
             def _():
-                for kind in (0, 1, 2):
-                    z_copy(kind, way, r).wait_send()
+                z_copy(2, way, r).wait_send()
+                for h in range(PIECES):
+                    z_copy(0, way, r, h).wait_send()
+                    z_copy(1, way, r, h).wait_send()
         for r in range(1, outer):
             @pl.when(mo >= r if way == 0 else mo + r < outer)
             def _():
-                r_copy(way, r).wait_send()
+                for h in range(PIECES):
+                    r_copy(way, r, h).wait_send()
     for b in range(outer):
         for d in range(1, inner):
             m_copy(b, d).wait_send()
@@ -629,7 +673,15 @@
     for k in range(3):
         w_copy(k).wait_send()
         g_copy(k).wait_send()
-        stores[k].wait()
+
+
+def store_kernel(*refs):
+    sem = refs[-1]
+    copies = [pltpu.make_async_copy(refs[k], refs[4 + k], sem.at[k]) for k in range(4)]
+    for c in copies:
+        c.start()
+    for c in copies:
+        c.wait()
 
 
 def fits(args):
@@ -652,21 +704,14 @@
     outer = size // inner
     slot = -(-3 * rows * top // (2 * size) // 16) * 16
     span = inner * slot
-    me = lax.axis_index("expert")
-    meta = jnp.concatenate([
-        jnp.pad(expert_ids.T.astype(F32), ((0, 8 - top), (0, 0)), constant_values=-1.0),
-        jnp.pad(gate_weights.T, ((0, 8 - top), (0, 0))),
-    ], axis=0)
-    which = jnp.arange(size, dtype=jnp.int32)
-    source = which // inner * inner + jnp.bitwise_xor(me % inner, which % inner)
-    order = (source[None, :] < source[:, None]).astype(BF16)
     dims = (size, outer, inner, rows, width, top, slot, shard)
     anywhere = pl.BlockSpec(memory_space=pl.ANY)
-    vmem = pl.BlockSpec(memory_space=pltpu.VMEM)
     dma = pltpu.SemaphoreType.DMA
     hop = outer - 1
     scratch = [
-        pltpu.VMEM((2, outer, rows, width), BF16),
+        pltpu.VMEM((top, rows), jnp.int32),
+        pltpu.VMEM((top, rows), F32),
+        pltpu.VMEM((2, outer, width, rows), BF16),
         pltpu.VMEM((outer, inner, 16, rows), F32),
         pltpu.VMEM((outer, span, rows), BF16),
         pltpu.VMEM((2, outer, span, width), BF16),
@@ -681,8 +726,8 @@
         pltpu.VMEM((3, 2 * shard, hid), BF16),
         pltpu.VMEM((2, width, CAP), BF16),
         pltpu.VMEM((2, CAP, hid), BF16),
-        pltpu.VMEM((2, hop, rows, width), BF16),
-        pltpu.VMEM((2, hop, rows, width), BF16),
+        pltpu.VMEM((2, hop, width, rows), BF16),
+        pltpu.VMEM((2, hop, width, rows), BF16),
         pltpu.VMEM((8, rows), F32),
         pltpu.VMEM((size, rows), F32),
         pltpu.VMEM((size, rows), F32),
@@ -690,24 +735,34 @@
         pltpu.VMEM((size, rows), F32),
         pltpu.VMEM((size, rows), F32),
         pltpu.VMEM((CAP, 128), F32),
-        dma((6,)), dma((2, 2, hop)), dma((2, 2, hop)),
+        pltpu.VMEM((width, rows), F32),
+        dma((7,)), dma((2, 2, hop, PIECES)), dma((2, 2, hop, PIECES)),
         dma((outer, inner)), dma((outer, inner)), dma((2, hop)), dma((2, hop)),
         dma((3, outer, inner)), dma((3, outer, inner)),
-        dma((3,)), dma((3,)), dma((2, hop)), dma((2, hop)), dma((3,)), dma((3,)), dma((3,)),
+        dma((3,)), dma((3,)), dma((2, hop, PIECES)), dma((2, hop, PIECES)), dma((3,)), dma((3,)),
         pltpu.SemaphoreType.REGULAR,
     ]
-    grad = jax.ShapeDtypeStruct(w_gate.shape, BF16)
-    mixed, gd, gg, gu = pl.pallas_call(
+    mixed = pltpu.VMEM((width, rows), BF16)
+    grad = pltpu.VMEM(w_gate.shape, BF16)
+    results = pl.pallas_call(
         functools.partial(step_kernel, dims),
-        out_shape=(jax.ShapeDtypeStruct((rows, width), BF16), grad, grad, grad),
-        in_specs=[anywhere, anywhere, anywhere, vmem, anywhere, anywhere, anywhere],
-        out_specs=(vmem, anywhere, anywhere, anywhere),
+        out_shape=(mixed, grad, grad, grad),
+        in_specs=[anywhere] * 7,
+        out_specs=(pl.BlockSpec(memory_space=pltpu.VMEM),) * 4,
         scratch_shapes=scratch,
         compiler_params=pltpu.CompilerParams(
-            collective_id=1, has_side_effects=True, vmem_limit_bytes=67043328
+            collective_id=1, has_side_effects=True, vmem_limit_bytes=56 << 20
         ),
-    )(tokens, cotangent, meta, order, w_gate, w_up, w_down)
-    return mixed, gg, gu, gd
+    )(tokens.T, cotangent.T, expert_ids.T, gate_weights.T, w_gate, w_up, w_down)
+    mixed, gd, gg, gu = pl.pallas_call(
+        store_kernel,
+        out_shape=tuple(jax.ShapeDtypeStruct(r.shape, r.dtype) for r in results),
+        in_specs=[pl.BlockSpec(memory_space=pltpu.VMEM)] * 4,
+        out_specs=(anywhere,) * 4,
+        scratch_shapes=[dma((4,))],
+        compiler_params=pltpu.CompilerParams(vmem_limit_bytes=1 << 20),
+    )(*[pltpu.with_memory_space_constraint(r, pltpu.VMEM) for r in results])
+    return mixed.T, gg, gu, gd
 
 
 def body(*args):

time: 131 us -> 97 us (0.74)
  Pallas kernels: 115 us -> 94.6 us
  local copies, waits for them, and re-layouts: 12.8 us -> 0 us
  other arithmetic: 2.64 us -> 0 us
    pallas_call x1 -> x2, Pallas kernels: 115 us -> 94.6 us  [the longest x1 91.6 us: fused_layer(): pl.pallas_call(functools.partial(step_kernel, dims), out_shape=(mixed, gr...]
    unnamed x10 -> x0, local copies, waits for them, and re-layouts: 12.8 us -> none
    convert_element_type x2 -> x0, other arithmetic: 1.35 us -> none  [the longest x1 0.69 us: fused_layer(): expert_ids.T.astype(F32)]
where the time goes in v1:
time: 97 us; the launch traced here: 95.4 us
  Pallas kernels  94.6 us (98%)
    pallas_call x1, Pallas kernels, fused_layer(): pl.pallas_call(functools.partial(step_kernel, dims), out_shape=(mixed, gr...  91.6 us
    pallas_call x1, Pallas kernels, fused_layer(): pl.pallas_call(store_kernel, out_shape=tuple((jax.ShapeDtypeStruct(r.shap...  2.97 us

profile of v1, /device:TPU:0, one launch (start us, length us, event | category | flops | bytes accessed | tf_op | source)
XLA Modules:
  0.0 95.4 jit_solution(6407923427385432024)
XLA Ops:
  0.6 91.6 %shard_map.102 = (bf16[1440,128]{1,0:T(8,128)(2,1)S(1)}, bf16[1,720,1440]{2,1,0:T(8,128)(2,1)S(1)}, bf16[1,720,1440]{2,1,0:T(8,128)(2,1)S(1)}, bf16[1,720,1440]{2,1,0:T(8,128)(2,1)S(1)}) custom-call(bf16[1440,128]{1,0:T(8,128)(2,1)} %bitcast.5, bf16[1440,128]{1,0:T(8,128)(2,1)} %bitcast.6, s32[4,128]{1,0:T(4,128)} %bitcast.7, f32[4,128]{1,0:T(4,128)} %bitcast.8, ...), custom_call_target="tpu_custom_call" | custom-call | tf_op jit(solution)/shard_map/pallas_call | solution.py:747
  92.2 3.0 %shard_map.103 = (bf16[1440,128]{1,0:T(8,128)(2,1)}, bf16[1,720,1440]{2,1,0:T(8,128)(2,1)}, bf16[1,720,1440]{2,1,0:T(8,128)(2,1)}, bf16[1,720,1440]{2,1,0:T(8,128)(2,1)}) custom-call(bf16[1440,128]{1,0:T(8,128)(2,1)S(1)} %get-tuple-element.12.refs_0_, bf16[1,720,1440]{2,1,0:T(8,128)(2,1)S(1)} %get-tuple-element.13.refs_1_, ...), custom_call_target="tpu_custom_call" | custom-call | tf_op jit(solution)/shard_map/pallas_call | solution.py:757

commit v2 on v1

--- a/solution.py
+++ b/solution.py
@@ -10,8 +10,10 @@
 
 CAP = 512
 INNER = 4
-TILE = 512
+TILE = 768
 PIECES = 2
+HOPS = 2
+STORES = 1
 SWISH_SLOPE = 1.702
 F32 = jnp.float32
 BF16 = jnp.bfloat16
@@ -220,12 +222,17 @@
 def step_kernel(
     dims, tok_in, cot_in, ids_in, gates_in, wg_in, wu_in, wd_in,
     mixed_out, gd_out, gg_out, gu_out,
-    ids_buf, gates_buf, col, meta, sel, send, recv, back, pack, x, act, out, g, coef, w, xt, dact,
-    zin, zout, near, mask, gq, start, count, place, row_gate, total,
+    ids_buf, gates_buf, col, meta, sel, selg, send, send_t, recv, recv_t, back, back_t, pack, packg,
+    x, act, out, out_t, g, coef, w, xt, dact,
+    zin, zout, near, mask, gq, start, count, place, row_gate, total, mixed,
     load_sem, z_send, z_recv, m_send, m_recv, ms_send, ms_recv, p_send, p_recv,
-    w_send, w_recv, r_send, r_recv, g_send, g_recv, free_sem,
+    w_send, w_recv, r_send, r_recv, g_send, g_recv, free_sem, o_sem,
 ):
     size, outer, inner, rows, width, top, slot, shard = dims
+    main = width // 128 * 128
+    rest = width - main
+    groups = slot // 16
+    few = inner * 16
     span = inner * slot
     me = lax.axis_index("expert")
     dp = lax.axis_index("dp")
@@ -241,16 +248,29 @@
             device_id=device, device_id_type=mesh_id,
         )
 
-    def tiles(fn):
-        full = width // TILE
+    def tiles(fn, end=width):
+        full = end // TILE
         if full:
             def step(i, carry):
                 fn(pl.ds(pl.multiple_of(i * TILE, TILE), TILE))
                 return carry
 
             lax.fori_loop(0, full, step, 0)
-        if width % TILE:
-            fn(pl.ds(full * TILE, width % TILE))
+        if end % TILE:
+            fn(pl.ds(full * TILE, end % TILE))
+
+    def repeat(t):
+        return jnp.concatenate([t] * (128 // rest), axis=0)
+
+    def lane_group(count, g):
+        lane = lax.broadcasted_iota(jnp.int32, (count, 128), 1)
+        return jnp.logical_and(lane >= g * rest, lane < (g + 1) * rest)
+
+    def fold(y, count):
+        out_rows = jnp.zeros((count, 128), F32)
+        for g in range(groups):
+            out_rows = jnp.where(lane_group(count, g), y[g * count:(g + 1) * count, :], out_rows)
+        return out_rows.astype(BF16)
 
     def zero_ends():
         for way, has in ((0, has_up), (1, has_dn)):
@@ -289,10 +309,8 @@
     zero_ends()
     for c in loads[2:]:
         c.wait()
-    meta[mo, 0, 0:8, :] = jnp.full((8, rows), -1.0, F32)
-    meta[mo, 0, 8:16, :] = jnp.zeros((8, rows), F32)
     meta[mo, 0, 0:top, :] = ids_buf[...].astype(F32)
-    meta[mo, 0, 8:8 + top, :] = gates_buf[...]
+    meta[mo, 0, top:2 * top, :] = gates_buf[...]
     for c in loads[:2]:
         c.wait()
     pl.semaphore_wait(
@@ -377,7 +395,7 @@
         return jnp.where(a < b, 1.0, 0.0).astype(BF16)
 
     def build(b):
-        ids = meta[b, 0, 0:8, :]
+        ids = meta[b, 0]
         named = jnp.zeros((8, rows), F32)
         for k in range(top):
             named = named + jnp.where(ids[k:k + 1, :] == near[...], 1.0, 0.0)
@@ -385,23 +403,46 @@
         spot = jnp.where(named > 0.0, rank, float(slot))
         within = lax.broadcasted_iota(jnp.int32, (slot, rows), 0).astype(F32)
         for d in range(inner):
-            sel[b, d * slot:(d + 1) * slot, :] = jnp.where(spot[d:d + 1, :] == within, 1.0, 0.0).astype(BF16)
+            hit = jnp.where(spot[d:d + 1, :] == within, 1.0, 0.0).astype(BF16)
+            sel[b, d * slot:(d + 1) * slot, :] = hit
+            for i in range(groups):
+                selg[b, i * few + d * 16:i * few + (d + 1) * 16, :] = hit[i * 16:(i + 1) * 16, :]
 
     def m_copy(b, d):
         return remote(meta.at[b, 0], meta.at[b, d], m_send.at[b, d], m_recv.at[b, d], {"expert": pal[d]})
 
     def p_copy(kind, b, d):
-        part = pl.ds(d * slot, slot)
-        dst = recv.at[kind, b, part] if kind < 2 else back.at[b, part]
-        src = send.at[kind, b, part] if kind < 2 else send.at[0, b, part]
-        return remote(src, dst, p_send.at[kind, b, d], p_recv.at[kind, b, d], {"expert": pal[d]})
+        part, little = pl.ds(d * slot, slot), pl.ds(d * 16, 16)
+        to = {"expert": pal[d]}
+        frm = kind if kind < 2 else 0
+        ends = (recv.at[kind, b, part], recv_t.at[kind, b, little]) if kind < 2 else (
+            back.at[b, part], back_t.at[b, little])
+        return (
+            remote(send.at[frm, b, part], ends[0], p_send.at[kind, b, d, 0], p_recv.at[kind, b, d, 0], to),
+            remote(send_t.at[frm, b, little], ends[1], p_send.at[kind, b, d, 1], p_recv.at[kind, b, d, 1], to),
+        )
+
+    def p_start(kind, b, d):
+        for c in p_copy(kind, b, d):
+            c.start()
+
+    def p_wait_recv(kind, b, d):
+        for c in p_copy(kind, b, d):
+            c.wait_recv()
+
+    def p_wait_send(kind, b, d):
+        for c in p_copy(kind, b, d):
+            c.wait_send()
 
     def scatter(kind, b):
-        picked = dot_nt(sel[b], col[kind, b]).astype(BF16)
+        picked = dot_nt(sel[b], col[kind, b, :main, :]).astype(BF16)
+        picked_t = fold(dot_nt(selg[b], repeat(col[kind, b, main:, :])), few)
         send[kind, b, slot:, :] = picked[slot:, :]
+        send_t[kind, b, 16:, :] = picked_t[16:, :]
         recv[kind, b, :slot, :] = picked[:slot, :]
+        recv_t[kind, b, :16, :] = picked_t[:16, :]
         for d in range(1, inner):
-            p_copy(kind, b, d).start()
+            p_start(kind, b, d)
 
     def spread_tok(b):
         for d in range(1, inner):
@@ -437,13 +478,17 @@
     for b in range(outer):
         for d in range(1, inner):
             m_copy(b, d).wait_recv()
-    mine = jnp.full((8, rows), me, jnp.int32).astype(F32)
+    mine = jnp.full((1, rows), me, jnp.int32).astype(F32)
     for b in range(outer):
         for d in range(inner):
             q = b * inner + d
-            same = meta[b, d, 0:8, :] == mine
-            mask[q:q + 1, :] = jnp.sum(jnp.where(same, 1.0, 0.0), axis=0, keepdims=True)
-            gq[q:q + 1, :] = jnp.sum(jnp.where(same, meta[b, d, 8:16, :], 0.0), axis=0, keepdims=True)
+            row, gate = jnp.zeros((1, rows), F32), jnp.zeros((1, rows), F32)
+            for k in range(top):
+                same = meta[b, d, k:k + 1, :] == mine
+                row = row + jnp.where(same, 1.0, 0.0)
+                gate = gate + jnp.where(same, meta[b, d, top + k:top + k + 1, :], 0.0)
+            mask[q:q + 1, :] = row
+            gq[q:q + 1, :] = gate
     held = mask[...].astype(BF16)
     first = jnp.bitwise_xor(lax.broadcasted_iota(jnp.int32, (size, size), 0), mi)
     second = jnp.bitwise_xor(lax.broadcasted_iota(jnp.int32, (size, size), 1), mi)
@@ -458,9 +503,12 @@
     for q in range(size):
         target = jnp.where(within < count[q:q + 1, :128], start[q:q + 1, :128] + within, float(CAP))
         for j in range(CAP // 128):
-            pack[q * slot:(q + 1) * slot, j * 128:(j + 1) * 128] = jnp.where(
-                target == lane + float(j * 128), 1.0, 0.0
-            ).astype(BF16)
+            hit = jnp.where(target == lane + float(j * 128), 1.0, 0.0).astype(BF16)
+            here = slice(j * 128, (j + 1) * 128)
+            pack[q * slot:(q + 1) * slot, here] = hit
+            b, d = q // inner, q % inner
+            for i in range(groups):
+                packg[i, b, d * 16:(d + 1) * 16, here] = hit[i * 16:(i + 1) * 16, :]
     down = lax.broadcasted_iota(jnp.int32, (128, rows), 0).astype(F32)
     for j in range(CAP // 128):
         acc = jnp.zeros((128, rows), F32)
@@ -468,19 +516,59 @@
             acc = acc + jnp.where(place[q:q + 1, :] == down + float(j * 128), gq[q:q + 1, :], 0.0)
         row_gate[j * 128:(j + 1) * 128, :] = jnp.broadcast_to(jnp.sum(acc, axis=1, keepdims=True), (128, 128))
 
+    low = jnp.logical_not(mo * 2 < outer).astype(jnp.int32)
+    last = (1 - low) * (outer - 1)
+
+    def arrive(kind, begin, n_blocks):
+        for i in range(n_blocks):
+            for d in range(1, inner):
+                p_wait_recv(kind, begin + i, d)
+
+    def gather(kind, begin, n_blocks, n):
+        from_rows = pl.ds(pl.multiple_of(begin * span, 16), n_blocks * span)
+        blocks = recv[kind, pl.ds(begin, n_blocks), :, n]
+        return dot_tn(pack[from_rows, :], blocks.reshape(n_blocks * span, n.size))
+
+    def gather_t(kind, begin, n_blocks):
+        n_few = n_blocks * few
+        held_t = recv_t[kind, pl.ds(begin, n_blocks)].reshape(n_few, 128).astype(F32)
+        wide = jnp.zeros((CAP, 128), F32)
+        for i in range(groups):
+            one = jnp.where(lane_group(n_few, i), held_t, 0.0).astype(BF16)
+            wide = wide + dot_tn(packg[i, pl.ds(begin, n_blocks)].reshape(n_few, CAP), one)
+        thin = wide[:, :rest]
+        for i in range(1, groups):
+            thin = thin + wide[:, i * rest:(i + 1) * rest]
+        return thin
+
+    def fill(kind, ref, gated):
+        def finish(v):
+            return (v * row_gate[:, :1] if gated else v).astype(BF16)
+
+        def early(n):
+            ref[:, n] = finish(gather(kind, low, outer - 1, n))
+
+        def late(n):
+            ref[:, n] = ref[:, n] + finish(gather(kind, last, 1, n))
+
+        def early_all():
+            tiles(early, main)
+            ref[:, main:] = finish(gather_t(kind, low, outer - 1))
+
+        def late_all():
+            tiles(late, main)
+            ref[:, main:] = ref[:, main:] + finish(gather_t(kind, last, 1))
+
+        return early_all, late_all
+
+    x_early, x_late = fill(0, x, False)
+    g_early, g_late = fill(1, g, True)
     cot_at(0, inside)
-    for b in range(outer):
-        for d in range(1, inner):
-            p_copy(0, b, d).wait_recv()
-
-    def gather(kind, n):
-        return dot_tn(pack[...], recv[kind, :, :, n].reshape(outer * span, n.size))
-
-    def pack_x(n):
-        x[:, n] = gather(0, n).astype(BF16)
-
-    tiles(pack_x)
+    arrive(0, low, outer - 1)
+    x_early()
+    arrive(0, last, 1)
     cot_at(0, at_end)
+    x_late()
     cot_at(1, inside)
 
     for k in (1, 2):
@@ -498,6 +586,7 @@
         coef[1, :, n] = value
 
     tiles(forward)
+    pl.semaphore_signal(free_sem.at[0], inc=1, device_id={"dp": other}, device_id_type=mesh_id)
     cot_at(1, at_end)
 
     w_loads[0].wait()
@@ -506,19 +595,23 @@
     def project(n):
         out[:, n] = (dot_nt(act[...], w[0, n, :]) * row_gate[:, :1]).astype(BF16)
 
-    tiles(project)
-
+    tiles(project, main)
+    out_t[...] = (dot_nt(act[...], repeat(w[0, main:, :])) * row_gate[:, :1]).astype(BF16)
     for b in range(outer):
         for d in range(1, inner):
-            p_copy(0, b, d).wait_send()
+            p_wait_send(0, b, d)
+
 
     def give_back(b):
         part = pl.ds(pl.multiple_of(b * span, 16), span)
         rows_back = dot(pack[part, :], out[...]).astype(BF16)
+        rows_t = fold(dot(packg[:, b].reshape(groups * few, CAP), out_t[...]), few)
         send[0, b, slot:, :] = rows_back[slot:, :]
+        send_t[0, b, 16:, :] = rows_t[16:, :]
         back[b, :slot, :] = rows_back[:slot, :]
+        back_t[b, :16, :] = rows_t[:16, :]
         for d in range(1, inner):
-            p_copy(2, b, d).start()
+            p_start(2, b, d)
 
     def give_round(r):
         @pl.when(mo >= r)
@@ -533,20 +626,30 @@
     give_round(outer - 1)
     for r in range(2, outer - 1):
         cot_round(r)
-    for r in range(outer - 2, -1, -1):
-        give_round(r)
+
+    @pl.when(inside)
+    def _():
+        for r in range(outer - 2, -1, -1):
+            give_round(r)
+
+
+    def strip(h):
+        return pl.ds(h * (width // HOPS), width // HOPS)
 
     def r_copy(way, r, h):
         to = me - inner if way == 0 else me + inner
         return remote(
-            zout.at[way, r - 1, piece(h)], zin.at[way, r - 1, piece(h)],
+            zout.at[way, r - 1, strip(h)], zin.at[way, r - 1, strip(h)],
             r_send.at[way, r - 1, h], r_recv.at[way, r - 1, h], {"expert": to},
         )
 
     def partial(b):
         for d in range(1, inner):
-            p_copy(2, b, d).wait_recv()
-        return dot_tn(back[b], sel[b])
+            p_wait_recv(2, b, d)
+        thin = jnp.zeros((rest, rows), F32)
+        for i in range(groups):
+            thin = thin + dot_tn(back_t[b], selg[b, i * few:(i + 1) * few, :])[i * rest:(i + 1) * rest, :]
+        return jnp.concatenate([dot_tn(back[b], sel[b]), thin], axis=0)
 
     def gives(way, r):
         return mo >= r if way == 0 else mo + r < outer
@@ -556,7 +659,7 @@
             @pl.when(gives(way, r))
             def _():
                 zout[way, r - 1] = partial(mo - r if way == 0 else mo + r).astype(BF16)
-        for h in range(PIECES):
+        for h in range(HOPS):
             for way, inbound in ((0, has_up), (1, has_dn)):
                 @pl.when(gives(way, r))
                 def _():
@@ -564,20 +667,25 @@
                         @pl.when(inbound)
                         def _():
                             r_copy(way, r + 1, h).wait_recv()
-                            zout[way, r - 1, piece(h)] = (
-                                zout[way, r - 1, piece(h)].astype(F32) + zin[way, r, piece(h)].astype(F32)
+                            zout[way, r - 1, strip(h)] = (
+                                zout[way, r - 1, strip(h)].astype(F32) + zin[way, r, strip(h)].astype(F32)
                             ).astype(BF16)
                     r_copy(way, r, h).start()
 
     def ret_last():
         total[...] = partial(mo)
-        for h in range(PIECES):
+        for b in range(outer):
+            for d in range(1, inner):
+                p_wait_send(2, b, d)
+        for k in range(3):
+            g_copy(k).wait_send()
+        for h in range(HOPS):
             for way, inbound in ((0, has_up), (1, has_dn)):
                 @pl.when(inbound)
                 def _():
                     r_copy(way, 1, h).wait_recv()
-            mixed_out[piece(h)] = (
-                total[piece(h)] + zin[0, 0, piece(h)].astype(F32) + zin[1, 0, piece(h)].astype(F32)
+            mixed[strip(h)] = (
+                total[strip(h)] + zin[0, 0, strip(h)].astype(F32) + zin[1, 0, strip(h)].astype(F32)
             ).astype(BF16)
 
     def flip_x(n):
@@ -589,68 +697,14 @@
         return jnp.where(a == b, 1.0, 0.0).astype(BF16)
 
     tiles(flip_x)
+    arrive(1, low, outer - 1)
+    g_early()
     ret_round(outer - 1)
 
-    for b in range(outer):
-        for d in range(1, inner):
-            p_copy(1, b, d).wait_recv()
-
-    def pack_g(n):
-        g[:, n] = (gather(1, n) * row_gate[:, :1]).astype(BF16)
-
-    tiles(pack_g)
-
-    def flip_g(n):
-        xt[0, n, :] = dot_tn(g[:, n], unit()).astype(BF16)
-
-    tiles(flip_g)
-
-    def back_act(n):
-        d_hidden = dot(g[...], w[0, :, n])
-        dact[0, :, n] = (d_hidden * coef[0, :, n]).astype(BF16)
-        dact[1, :, n] = (d_hidden * coef[1, :, n]).astype(BF16)
-
-    tiles(back_act)
-    pl.semaphore_signal(free_sem, inc=1, device_id={"dp": other}, device_id_type=mesh_id)
-
-    send_rows = pl.ds(0, shard)
-    recv_rows = pl.ds(shard, shard)
-
-    def g_copy(k):
-        return remote(
-            w.at[k, send_rows], w.at[k, recv_rows], g_send.at[k], g_recv.at[k], {"dp": other}
-        )
-
-    def right(k, n):
-        return act[:, n] if k == 0 else dact[k - 1, :, n]
-
-    their_rows = pl.ds(pl.multiple_of(other * shard, 16), shard)
-    for r in range(outer - 2, 1, -1):
-        ret_round(r)
-    for k in range(3):
-        lhs = 0 if k == 0 else 1
-
-        def theirs(n):
-            w[k, send_rows, n] = dot(xt[lhs, their_rows, :], right(k, n)).astype(BF16)
-
-        tiles(theirs)
-        if k == 0:
-            pl.semaphore_wait(free_sem, 1)
-        g_copy(k).start()
-    if outer > 2:
-        ret_round(1)
-    outs = (gd_out, gg_out, gu_out)
-    for k in range(3):
-        lhs = 0 if k == 0 else 1
-        g_copy(k).wait_recv()
-
-        def ours(n):
-            grad = dot(xt[lhs, own_rows, :], right(k, n)) + w[k, recv_rows, n].astype(F32)
-            outs[k][0, :, n] = grad.astype(BF16)
-
-        tiles(ours)
-
-    ret_last()
+    @pl.when(at_end)
+    def _():
+        for r in range(outer - 2, -1, -1):
+            give_round(r)
 
     for way in (0, 1):
         for r in range(outer - 1):
@@ -660,37 +714,122 @@
                 for h in range(PIECES):
                     z_copy(0, way, r, h).wait_send()
                     z_copy(1, way, r, h).wait_send()
-        for r in range(1, outer):
-            @pl.when(mo >= r if way == 0 else mo + r < outer)
-            def _():
-                for h in range(PIECES):
-                    r_copy(way, r, h).wait_send()
+    for k in range(3):
+        w_copy(k).wait_send()
     for b in range(outer):
         for d in range(1, inner):
             m_copy(b, d).wait_send()
-            p_copy(1, b, d).wait_send()
-            p_copy(2, b, d).wait_send()
+    for i in range(outer - 1):
+        for d in range(1, inner):
+            p_wait_send(1, low + i, d)
+    arrive(1, last, 1)
+    for d in range(1, inner):
+        p_wait_send(1, last, d)
+
+    g_late()
+
+    def flip_g(n):
+        xt[0, n, :] = dot_tn(g[:, n], unit()).astype(BF16)
+
+    tiles(flip_g)
+
+    spot_of = (1, 2, 0)
+    send_rows = pl.ds(0, shard)
+    recv_rows = pl.ds(shard, shard)
+
+    def g_copy(k):
+        return remote(
+            w.at[spot_of[k], send_rows], w.at[spot_of[k], recv_rows], g_send.at[k], g_recv.at[k], {"dp": other}
+        )
+
+    def right(k, n):
+        return act[:, n] if k == 0 else dact[k - 1, :, n]
+
+    their_rows = pl.ds(pl.multiple_of(other * shard, 16), shard)
+
+    def send_theirs(k):
+        def theirs(n):
+            w[spot_of[k], send_rows, n] = dot(xt[min(k, 1), their_rows, :], right(k, n)).astype(BF16)
+
+        tiles(theirs)
+        g_copy(k).start()
+
+    pl.semaphore_wait(free_sem.at[0], 1)
+    send_theirs(0)
+
+    def back_act(n):
+        d_hidden = dot(g[...], w[0, :, n])
+        dact[0, :, n] = (d_hidden * coef[0, :, n]).astype(BF16)
+        dact[1, :, n] = (d_hidden * coef[1, :, n]).astype(BF16)
+
+    tiles(back_act)
+    pl.semaphore_signal(free_sem.at[1], inc=1, device_id={"dp": other}, device_id_type=mesh_id)
+
+    for r in range(outer - 2, 1, -1):
+        ret_round(r)
+    send_theirs(1)
+    pl.semaphore_wait(free_sem.at[1], 1)
+    send_theirs(2)
+    if outer > 2:
+        ret_round(1)
+    outs = (gd_out, gg_out, gu_out)
+    stores = []
     for k in range(3):
-        w_copy(k).wait_send()
-        g_copy(k).wait_send()
+        lhs = 0 if k == 0 else 1
+        g_copy(k).wait_recv()
+
+        def ours(n):
+            grad = dot(xt[lhs, own_rows, :], right(k, n)) + w[spot_of[k], recv_rows, n].astype(F32)
+            w[spot_of[k], recv_rows, n] = grad.astype(BF16)
+
+        tiles(ours)
+        store = pltpu.make_async_copy(w.at[spot_of[k], recv_rows], outs[k].at[0], o_sem.at[k])
+        store.start()
+        stores.append(store)
+    ret_last()
+    stores.append(pltpu.make_async_copy(mixed, mixed_out, o_sem.at[3]))
+    stores[3].start()
+
+    for way in (0, 1):
+        for r in range(1, outer):
+            @pl.when(gives(way, r))
+            def _():
+                for h in range(HOPS):
+                    r_copy(way, r, h).wait_send()
+    for store in stores:
+        store.wait()
 
 
 def store_kernel(*refs):
     sem = refs[-1]
-    copies = [pltpu.make_async_copy(refs[k], refs[4 + k], sem.at[k]) for k in range(4)]
+    copies = []
+    for k in range(4):
+        src, dst = refs[k], refs[4 + k]
+        if k > 0:
+            src, dst = src.at[0], dst.at[0]
+        step = src.shape[0] // STORES
+        for i in range(STORES):
+            part = pl.ds(i * step, step)
+            copies.append(pltpu.make_async_copy(src.at[part], dst.at[part], sem.at[k, i]))
     for c in copies:
         c.start()
     for c in copies:
         c.wait()
 
 
+def slots(args):
+    rows, top = args[2].shape
+    return -(-3 * rows * top // (2 * lax.axis_size("expert")) // 16) * 16
+
+
 def fits(args):
-    rows = args[0].shape[0]
+    rows, width = args[0].shape
     shard = args[4].shape[1]
     size = lax.axis_size("expert")
     return (
-        lax.axis_size("dp") == 2 and shard % 16 == 0 and rows == 128
+        lax.axis_size("dp") == 2 and args[2].shape[1] == 4 and shard % 16 == 0 and rows == 128
         and size % INNER == 0 and INNER < size <= 16
+        and width % 128 in (32, 64) and slots(args) // 16 * (width % 128) <= 128
     )
 
 
@@ -702,8 +841,9 @@
     hid = w_gate.shape[2]
     inner = INNER
     outer = size // inner
-    slot = -(-3 * rows * top // (2 * size) // 16) * 16
+    slot = slots((tokens, cotangent, expert_ids))
     span = inner * slot
+    main, few = width // 128 * 128, inner * 16
     dims = (size, outer, inner, rows, width, top, slot, shard)
     anywhere = pl.BlockSpec(memory_space=pl.ANY)
     dma = pltpu.SemaphoreType.DMA
@@ -712,15 +852,21 @@
         pltpu.VMEM((top, rows), jnp.int32),
         pltpu.VMEM((top, rows), F32),
         pltpu.VMEM((2, outer, width, rows), BF16),
-        pltpu.VMEM((outer, inner, 16, rows), F32),
+        pltpu.VMEM((outer, inner, 2 * top, rows), F32),
         pltpu.VMEM((outer, span, rows), BF16),
-        pltpu.VMEM((2, outer, span, width), BF16),
-        pltpu.VMEM((2, outer, span, width), BF16),
-        pltpu.VMEM((outer, span, width), BF16),
+        pltpu.VMEM((outer, span, rows), BF16),
+        pltpu.VMEM((2, outer, span, main), BF16),
+        pltpu.VMEM((2, outer, few, 128), BF16),
+        pltpu.VMEM((2, outer, span, main), BF16),
+        pltpu.VMEM((2, outer, few, 128), BF16),
+        pltpu.VMEM((outer, span, main), BF16),
+        pltpu.VMEM((outer, few, 128), BF16),
         pltpu.VMEM((outer * span, CAP), BF16),
+        pltpu.VMEM((slot // 16, outer, few, CAP), BF16),
         pltpu.VMEM((CAP, width), BF16),
         pltpu.VMEM((CAP, hid), BF16),
-        pltpu.VMEM((CAP, width), BF16),
+        pltpu.VMEM((CAP, main), BF16),
+        pltpu.VMEM((CAP, 128), BF16),
         pltpu.VMEM((CAP, width), BF16),
         pltpu.VMEM((2, CAP, hid), F32),
         pltpu.VMEM((3, 2 * shard, hid), BF16),
@@ -736,11 +882,12 @@
         pltpu.VMEM((size, rows), F32),
         pltpu.VMEM((CAP, 128), F32),
         pltpu.VMEM((width, rows), F32),
+        pltpu.VMEM((width, rows), BF16),
         dma((7,)), dma((2, 2, hop, PIECES)), dma((2, 2, hop, PIECES)),
         dma((outer, inner)), dma((outer, inner)), dma((2, hop)), dma((2, hop)),
-        dma((3, outer, inner)), dma((3, outer, inner)),
-        dma((3,)), dma((3,)), dma((2, hop, PIECES)), dma((2, hop, PIECES)), dma((3,)), dma((3,)),
-        pltpu.SemaphoreType.REGULAR,
+        dma((3, outer, inner, 2)), dma((3, outer, inner, 2)),
+        dma((3,)), dma((3,)), dma((2, hop, HOPS)), dma((2, hop, HOPS)), dma((3,)), dma((3,)),
+        pltpu.SemaphoreType.REGULAR((2,)), dma((4,)),
     ]
     mixed = pltpu.VMEM((width, rows), BF16)
     grad = pltpu.VMEM(w_gate.shape, BF16)
@@ -748,7 +895,7 @@
         functools.partial(step_kernel, dims),
         out_shape=(mixed, grad, grad, grad),
         in_specs=[anywhere] * 7,
-        out_specs=(pl.BlockSpec(memory_space=pltpu.VMEM),) * 4,
+        out_specs=(anywhere,) * 4,
         scratch_shapes=scratch,
         compiler_params=pltpu.CompilerParams(
             collective_id=1, has_side_effects=True, vmem_limit_bytes=56 << 20
@@ -759,7 +906,7 @@
         out_shape=tuple(jax.ShapeDtypeStruct(r.shape, r.dtype) for r in results),
         in_specs=[pl.BlockSpec(memory_space=pltpu.VMEM)] * 4,
         out_specs=(anywhere,) * 4,
-        scratch_shapes=[dma((4,))],
+        scratch_shapes=[dma((4, STORES))],
         compiler_params=pltpu.CompilerParams(vmem_limit_bytes=1 << 20),
     )(*[pltpu.with_memory_space_constraint(r, pltpu.VMEM) for r in results])
     return mixed.T, gg, gu, gd

time: 97 us -> 95.1 us (0.980)
  Pallas kernels: 94.6 us -> 93.1 us
    pallas_call x1, Pallas kernels: 91.6 us -> 90.1 us  [fused_layer(): pl.pallas_call(functools.partial(step_kernel, dims), out_shape=(mixed, gr...]
where the time goes in v2:
time: 95.1 us; the launch traced here: 93.9 us
  Pallas kernels  93.1 us (98%)
    pallas_call x1, Pallas kernels, fused_layer(): pl.pallas_call(functools.partial(step_kernel, dims), out_shape=(mixed, gr...  90.1 us
    pallas_call x1, Pallas kernels, fused_layer(): pl.pallas_call(store_kernel, out_shape=tuple((jax.ShapeDtypeStruct(r.shap...  2.97 us

profile of v2, /device:TPU:0, one launch (start us, length us, event | category | flops | bytes accessed | tf_op | source)
XLA Modules:
  0.0 93.9 jit_solution(1487502627471765195)
XLA Ops:
  0.6 90.1 %shard_map.102 = (bf16[1440,128]{1,0:T(8,128)(2,1)S(1)}, bf16[1,720,1440]{2,1,0:T(8,128)(2,1)S(1)}, bf16[1,720,1440]{2,1,0:T(8,128)(2,1)S(1)}, bf16[1,720,1440]{2,1,0:T(8,128)(2,1)S(1)}) custom-call(bf16[1440,128]{1,0:T(8,128)(2,1)} %bitcast.5, bf16[1440,128]{1,0:T(8,128)(2,1)} %bitcast.6, s32[4,128]{1,0:T(4,128)} %bitcast.7, f32[4,128]{1,0:T(4,128)} %bitcast.8, ...), custom_call_target="tpu_custom_call" | custom-call | tf_op jit(solution)/shard_map/pallas_call | solution.py:894
  90.8 3.0 %shard_map.103 = (bf16[1440,128]{1,0:T(8,128)(2,1)}, bf16[1,720,1440]{2,1,0:T(8,128)(2,1)}, bf16[1,720,1440]{2,1,0:T(8,128)(2,1)}, bf16[1,720,1440]{2,1,0:T(8,128)(2,1)}) custom-call(bf16[1440,128]{1,0:T(8,128)(2,1)S(1)} %get-tuple-element.12.refs_0_, bf16[1,720,1440]{2,1,0:T(8,128)(2,1)S(1)} %get-tuple-element.13.refs_1_, ...), custom_call_target="tpu_custom_call" | custom-call | tf_op jit(solution)/shard_map/pallas_call | solution.py:904
